TPU v7x, 32 devices: a whole 2x2x4 slice. The times are simulated.
32 devices in a mesh: replica: 2 (over x), tp: 16 (over z, y, core).
Axes of the slice: x: 2, y: 2, z: 4, core: 2. Of those that a mesh axis runs over, the one named last changes fastest.
Arguments:
- tokens: bfloat16 [64, 16384], P('replica', 'tp'), parts along dimension 0, may hold values from -90 to 90
- in_gain: bfloat16 [16384], replicated, may hold values from 0.5 to 1.5
- w_query: bfloat16 [16384, 8192], P(None, 'tp'), may hold values from -0.046875 to 0.046875
- w_key: bfloat16 [16384, 1024], P('tp'), may hold values from -0.09375 to 0.09375
- w_value: bfloat16 [16384, 1024], P('tp'), may hold values from -0.046875 to 0.046875
- w_out: bfloat16 [8192, 16384], P('tp'), may hold values from -0.09375 to 0.09375
- cache_keys: bfloat16 [64, 256, 1024], P('replica', 'tp'), parts along dimension 0, may hold values from -910 to 910
- cache_values: bfloat16 [64, 256, 1024], P('replica', 'tp'), parts along dimension 0, may hold values from -24 to 24
- lengths: int32 [64], P('replica'), parts along dimension 0, may hold values from 1 to 255, as said below
- post_gain: bfloat16 [16384], P('tp'), may hold values from 0.5 to 1.5
Outputs:
- hidden: bfloat16 [64, 16384], P('replica', 'tp'), parts along dimension 0
- normed: bfloat16 [64, 16384], P('replica', 'tp'), parts along dimension 0
There are 2 independent parts, one for each index of `replica`. A program takes and returns all parts, laid end to end along the dimension named above; an argument that names none is the same for every part. Nothing has to cross between parts.
Inputs may be any that keep to these rules, and one draw needn't show every extreme that they name: `lengths`: positions already cached for each sequence; in every draw one sequence has exactly 255 and one has 8 or fewer.
All inputs are finite; a program needn't handle non-finite values.
Results may differ from a plain program's by a relative error of at most 0.019.
Values may be sent and summed in bfloat16 or wider, within the bound.
A program may use at most 128 MiB of HBM per device.

v0:
```python
import math
import jax
import jax.numpy as jnp
from jax import lax
from jax.sharding import PartitionSpec as P

HEADS = 64
KVH = 8
HD = 128
epsilon = 1e-05
rotary_base = 500000.0
masked_value = -1e30


def rotate(vectors, positions):
    half_size = vectors.shape[-1] // 2
    exponents = jnp.arange(half_size, dtype=jnp.float32) * (2.0 / vectors.shape[-1])
    frequency = jnp.power(jnp.float32(rotary_base), -exponents)
    angles = positions.astype(jnp.float32)[:, None] * frequency[None, :]
    cosine = jnp.cos(angles)[:, None, :]
    sine_part = jnp.sin(angles)[:, None, :]
    leading = vectors[..., :half_size]
    trailing = vectors[..., half_size:]
    return jnp.concatenate(
        [leading * cosine - trailing * sine_part, trailing * cosine + leading * sine_part], axis=-1
    )


def inverse_rms(rows_wide):
    return lax.rsqrt(jnp.mean(rows_wide * rows_wide, axis=-1, keepdims=True) + epsilon)


def local(
    tokens, in_gain, w_query, w_key, w_value, w_out, cache_keys, cache_values, lengths, post_gain
):
    device_rank = lax.axis_index("tp")
    batch_rows = tokens.shape[0]
    width_dev = tokens.shape[1]
    heads_dev = w_query.shape[1] // HD
    group_size = HEADS // KVH
    positions_dev = cache_keys.shape[1]
    score_scale = 1.0 / math.sqrt(HD)
    gathered = lax.all_gather(tokens, "tp", axis=1, tiled=True)
    residual = gathered.astype(jnp.float32)
    normed_in = (residual * inverse_rms(residual) * in_gain.astype(jnp.float32)).astype(
        jnp.bfloat16
    )
    own_rows = lax.dynamic_slice_in_dim(normed_in, device_rank * width_dev, width_dev, 1)
    key_part = jnp.dot(own_rows, w_key, preferred_element_type=jnp.float32)
    value_part = jnp.dot(own_rows, w_value, preferred_element_type=jnp.float32)
    key_sum, value_sum = lax.psum((key_part, value_part), "tp")
    fresh_key = rotate(key_sum.reshape(batch_rows, KVH, HD), lengths).astype(jnp.bfloat16)
    fresh_value = value_sum.astype(jnp.bfloat16).reshape(batch_rows, KVH, HD)
    query_wide = jnp.dot(normed_in, w_query, preferred_element_type=jnp.float32)
    own_query = rotate(query_wide.reshape(batch_rows, heads_dev, HD), lengths).astype(jnp.bfloat16)
    all_query = lax.all_gather(
        own_query.reshape(batch_rows, heads_dev * HD), "tp", axis=1, tiled=True
    )
    grouped = all_query.reshape(batch_rows, KVH, group_size, HD)
    cached_keys = cache_keys.reshape(batch_rows, positions_dev, KVH, HD)
    cached_values = cache_values.reshape(batch_rows, positions_dev, KVH, HD)
    scores = (
        jnp.einsum("bgqd,bpgd->bgqp", grouped, cached_keys, preferred_element_type=jnp.float32)
        * score_scale
    )
    positions = device_rank * positions_dev + jnp.arange(positions_dev, dtype=jnp.int32)
    visible = (positions[None, :] < lengths[:, None])[:, None, None, :]
    masked = jnp.where(visible, scores, masked_value)
    first_head = device_rank * heads_dev
    shared_head = first_head // group_size
    local_value = lax.dynamic_slice_in_dim(fresh_value, shared_head, 1, 1).astype(jnp.float32)
    fresh_scores = (
        jnp.einsum("bgqd,bgd->bgq", grouped, fresh_key, preferred_element_type=jnp.float32)
        * score_scale
    )
    cache_peak = lax.pmax(jnp.max(masked, axis=-1), "tp")
    overall_all = jnp.maximum(cache_peak, fresh_scores)
    weights = jnp.where(visible, jnp.exp(masked - overall_all[..., None]), 0.0)
    partial_value = jnp.einsum(
        "bgqp,bpgd->bgqd",
        weights.astype(jnp.bfloat16),
        cached_values,
        preferred_element_type=jnp.float32,
    )
    weighted, mass_sum = (
        lax.psum_scatter(
            partial_value.reshape(batch_rows, HEADS, HD), "tp", scatter_dimension=1, tiled=True
        ),
        lax.psum_scatter(
            jnp.sum(weights, axis=-1).reshape(batch_rows, HEADS),
            "tp",
            scatter_dimension=1,
            tiled=True,
        ),
    )
    own_fresh = lax.dynamic_slice_in_dim(
        fresh_scores.reshape(batch_rows, HEADS), first_head, heads_dev, 1
    )
    own_overall = lax.dynamic_slice_in_dim(
        overall_all.reshape(batch_rows, HEADS), first_head, heads_dev, 1
    )
    fresh_weight = jnp.exp(own_fresh - own_overall)
    denominator = mass_sum + fresh_weight
    rounded_fresh = lax.optimization_barrier(fresh_weight.astype(jnp.bfloat16)).astype(jnp.float32)
    weighted = weighted + rounded_fresh[..., None] * local_value
    head_rows = (
        (weighted / denominator[..., None]).astype(jnp.bfloat16).reshape(batch_rows, heads_dev * HD)
    )
    projected = jnp.dot(head_rows, w_out, preferred_element_type=jnp.float32)
    summed = lax.psum(projected, "tp")
    hidden_full = (residual + summed).astype(jnp.bfloat16)
    hidden = lax.dynamic_slice_in_dim(hidden_full, device_rank * width_dev, width_dev, 1)
    row_scale = inverse_rms(hidden_full.astype(jnp.float32))
    normed = (hidden.astype(jnp.float32) * row_scale * post_gain.astype(jnp.float32)).astype(
        jnp.bfloat16
    )
    return (hidden, normed)


def solution(mesh):
    placed = (
        P("replica", "tp"),
        P(),
        P(None, "tp"),
        P("tp", None),
        P("tp", None),
        P("tp", None),
        P("replica", "tp", None),
        P("replica", "tp", None),
        P("replica"),
        P("tp"),
    )
    return jax.shard_map(
        local,
        mesh=mesh,
        in_specs=placed,
        out_specs=(P("replica", "tp"), P("replica", "tp")),
        check_vma=False,
    )
```

profile of v0, /device:TPU:0, one launch (start us, length us, event | category | flops | bytes accessed | tf_op | source)
XLA Modules:
  0.0 332.5 jit_solution(15112100201063493515)
XLA Ops:
  7.2 0.7 all-gather.2.cloned.1.call-update
  8.0 0.8 convert_element_type.51
  9.4 0.7 broadcast_compare_fusion
  10.3 40.5 %all-gather.2.cloned.1.call-done = bf16[32,16384]{1,0:T(8,128)(2,1)} async-done(((bf16[32,1024]{1,0:T(8,128)(2,1)}), bf16[32,16384]{1,0:T(8,128)(2,1)}) %all-gather.2.cloned.1.call-update) | async-done | bytes 1048592 | tf_op jit(solution)/shard_map/all_gather | solution.py:43
  50.8 1.5 fusion
  52.3 1.5 fusion.2
  54.4 0.7 copy.39
  55.1 8.7 %fusion.31 = f32[32,512]{1,0:T(8,128)S(1)} fusion(bf16[32,16384]{1,0:T(8,128)(2,1)S(1)} %fusion.2, bf16[16384,512]{1,0:T(8,128)(2,1)} %param.12), kind=kOutput, calls=%fused_computation.59 | convolution fusion | flops 536870912 | bytes 17891328 | tf_op jit(solution)/shard_map/dot_general | solution.py:54
  64.2 21.0 %all_gather.7 = bf16[32,8192]{1,0:T(8,128)(2,1)S(1)} all-gather(bf16[32,512]{1,0:T(8,128)(2,1)S(1)} %bitcast.62), channel_id=1, replica_groups=mesh['replica'=2,'tp'=16] {'tp'}, dimensions={1}, use_global_device_ids=true | all-gather | bytes 557056 | tf_op jit(solution)/shard_map/all_gather | solution.py:56
  85.3 0.8 copy-done.3
  86.0 0.7 fusion.30
  86.8 58.8 %pmax.7 = f32[32,8,8]{2,1,0:T(8,128)S(1)} all-reduce(f32[32,8,8]{2,1,0:T(8,128)S(1)} %get-tuple-element.18), channel_id=1, replica_groups=mesh['replica'=2,'tp'=16] {'tp'}, use_global_device_ids=true, to_apply=%region_2.0 | all-reduce | flops 2048 | bytes 16384 | tf_op jit(solution)/shard_map/pmax | solution.py:76
  145.6 1.2 subtract_convert_fusion
  146.9 1.4 fusion.15
  149.6 1.6 copy.27
  152.5 2.1 fusion.17
  154.6 0.7 copy.29
  156.1 59.6 %all-reduce.9 = (f32[32,64]{0,1:T(8,128)S(1)}, bf16[32,1024]{1,0:T(8,128)(2,1)S(1)}) all-reduce(f32[32,64]{0,1:T(8,128)S(1)} %bitcast.60, f32[32,1024]{1,0:T(8,128)S(1)} %fusion.17), channel_id=3, replica_groups=mesh['replica'=2,'tp'=16] {'tp'}, use_global_device_ids=true, to_apply=%region_7.8.clone | all-reduce | flops 34816 | bytes 212992
  215.7 1.0 copy.28
  216.7 0.7 fusion.27
  217.4 10.2 %fusion.20 = f32[32,16384]{1,0:T(8,128)} fusion(bf16[512,16384]{1,0:T(8,128)(2,1)} %param.15, f32[32,4]{0,1:T(4,128)S(1)} %get-tuple-element.15, f32[32,4,128]{2,0,1:T(8,128)} %reduce-scatter.2.cloned.1.call-done, f32[32,128]{1,0:T(8,128)S(1)} %bitcast.59, f32[32,4]{0,1:T(4,128)S(1)} %convert_element_type.57), kind=kOutput, calls=%fused_computation.37 | convolution fusion | flops 536936448 | bytes 18957312 | tf_op jit(solution)/shard_map/dot_general | solution.py:109
  228.4 94.9 %all-reduce.8.cloned.1.call-done = f32[32,16384]{1,0:T(8,128)} async-done(((f32[32,16384]{1,0:T(8,128)}), f32[32,16384]{1,0:T(8,128)}) %all-reduce.8.cloned.1.call-update) | async-done | bytes 2097168 | tf_op jit(solution)/shard_map/psum | solution.py:110
  323.3 2.0 multiply_reduce_fusion
  325.3 0.7 multiply_convert_fusion
  (46 shorter events, 5.3 us)
Async XLA Ops:
  7.2 46.7 %copy-start = (bf16[1024,1024]{1,0:T(8,128)(2,1)S(1)}, bf16[1024,1024]{1,0:T(8,128)(2,1)}, u32[]{:S(2)}) copy-start(bf16[1024,1024]{1,0:T(8,128)(2,1)} %param.13) | copy-start | bytes 6291460
  7.2 43.6 %all-gather.2.cloned.1.call-start = ((), (), s32[]{:S(2)}) async-start(), calls=%async_computation.1 | async-start | bytes 1114112 | tf_op jit(solution)/shard_map/all_gather | solution.py:43
  7.9 137.7 %all-reduce.6.cloned.1.call-start = ((), (), s32[]{:S(2)}) async-start(), calls=%async_computation.2 | async-start | bytes 262144 | tf_op jit(solution)/shard_map/psum | solution.py:51
  53.9 10.0 %copy-start.2 = (bf16[32,16384]{1,0:T(8,128)(2,1)}, bf16[32,16384]{1,0:T(8,128)(2,1)S(1)}, u32[]{:S(2)}) copy-start(bf16[32,16384]{1,0:T(8,128)(2,1)S(1)} %fusion.2) | copy-start | bytes 3145732
  55.1 162.4 %reduce-scatter.2.cloned.1.call-start = ((), (), s32[]{:S(2)}) async-start(), calls=%async_computation.3 | async-start | bytes 1114112 | tf_op jit(solution)/shard_map/reduce_scatter | solution.py:86
  63.9 22.1 %copy-start.4 = (bf16[32,16,1024]{2,1,0:T(8,128)(2,1)S(1)}, bf16[32,16,1024]{2,1,0:T(8,128)(2,1)}, u32[]{:S(2)}) copy-start(bf16[32,16,1024]{2,1,0:T(8,128)(2,1)} %param.16) | copy-start | bytes 3145732
  85.3 0.8 copy-start.3
  145.6 3.4 %copy-start.5 = (bf16[32,16,1024]{2,1,0:T(8,128)(2,1)S(1)}, bf16[32,16,1024]{2,1,0:T(8,128)(2,1)}, u32[]{:S(2)}) copy-start(bf16[32,16,1024]{2,1,0:T(8,128)(2,1)} %param.17) | copy-start | bytes 3145732
  149.5 1.7 copy-start.7
  151.2 172.1 %all-reduce.8.cloned.1.call-start = ((), (), s32[]{:S(2)}) async-start(), calls=%async_computation.4 | async-start | bytes 4194304 | tf_op jit(solution)/shard_map/psum | solution.py:110
  227.7 0.7 copy-start.6
  227.7 95.6 %copy-start.1 = (bf16[32,16384]{1,0:T(8,128)(2,1)S(1)}, bf16[32,16384]{1,0:T(8,128)(2,1)}, u32[]{:S(2)}) copy-start(bf16[32,16384]{1,0:T(8,128)(2,1)} %all-gather.2.cloned.1.call-done) | copy-start | bytes 3145732
Sparse Core Ops, SparseCore 0:
  10.2 40.5 all-gather.1
  55.2 87.4 all-reduce.5
  151.3 56.5 reduce-scatter.1
  227.8 95.3 all-reduce.7
where the time goes:
time: 333 us
  blocking collectives  139 us (42%)
  waiting for transfers between devices  136 us (41%)
  matrix products  24.2 us (7%)
  between operations  14.6 us (4%)
  other arithmetic  11.6 us (3%)
  local copies, waits for them, and re-layouts  6.35 us (2%)
    psum x1, waiting for transfers between devices, local(): summed = lax.psum(projected, 'tp')  94.9 us
    unnamed x1, blocking collectives  59.6 us
    pmax x1, blocking collectives, local(): cache_peak = lax.pmax(jnp.max(masked, axis=-1), 'tp')  58.8 us
    all_gather x1, waiting for transfers between devices, local(): gathered = lax.all_gather(tokens, 'tp', axis=1, tiled=True)  40.5 us
    all_gather x1, blocking collectives, local(): lax.all_gather(own_query.reshape(batch_rows, heads_dev * HD), 'tp', axis=...  21 us
    dot_general x1, matrix products, local(): projected = jnp.dot(head_rows, w_out, preferred_element_type=jnp.float32)  10.2 us
    dot_general x1, matrix products, local(): query_wide = jnp.dot(normed_in, w_query, preferred_element_type=jnp.float32)  8.74 us
  transfers between devices with their start and end apart: 4, of which 2 were waited for; matrix products, arithmetic and copies ran while one was open for 5% of the time, Pallas kernels for 0%

commit v1 on v0

--- a/solution.py
+++ b/solution.py
@@ -107,7 +107,9 @@
         (weighted / denominator[..., None]).astype(jnp.bfloat16).reshape(batch_rows, heads_dev * HD)
     )
     projected = jnp.dot(head_rows, w_out, preferred_element_type=jnp.float32)
-    summed = lax.psum(projected, "tp")
+    summed = projected
+    for hop in (1, 2, 4, 8):
+        summed = summed + lax.ppermute(summed, "tp", [(dev, dev ^ hop) for dev in range(16)])
     hidden_full = (residual + summed).astype(jnp.bfloat16)
     hidden = lax.dynamic_slice_in_dim(hidden_full, device_rank * width_dev, width_dev, 1)
     row_scale = inverse_rms(hidden_full.astype(jnp.float32))

time: 333 us -> 426 us (1.28)
  waiting for transfers between devices: 136 us -> 232 us
    ppermute x0 -> x4, waiting for transfers between devices: none -> 190 us  [local(): lax.ppermute(summed, 'tp', [(dev, dev ^ hop) for dev in range(16)])]
    psum x1 -> x0, waiting for transfers between devices: 94.9 us -> none  [local(): summed = lax.psum(projected, 'tp')]
  transfers between devices with their start and end apart: 4 -> 7, of which waited for: 2 -> 5; matrix products, arithmetic and copies ran while one was open for 5% -> 4% of each run, Pallas kernels for 0% -> 0%
where the time goes in v1:
time: 426 us; the launch traced here: 425 us
  waiting for transfers between devices  232 us (54%)
  blocking collectives  139 us (33%)
  matrix products  22.9 us (5%)
  between operations  14.7 us (3%)
  other arithmetic  10.9 us (3%)
  local copies, waits for them, and re-layouts  5.72 us (1%)
    ppermute x4, waiting for transfers between devices, local(): lax.ppermute(summed, 'tp', [(dev, dev ^ hop) for dev in range(16)])  190 us
    unnamed x1, blocking collectives  59.6 us
    pmax x1, blocking collectives, local(): cache_peak = lax.pmax(jnp.max(masked, axis=-1), 'tp')  58.8 us
    all_gather x1, waiting for transfers between devices, local(): gathered = lax.all_gather(tokens, 'tp', axis=1, tiled=True)  40.5 us
    all_gather x1, blocking collectives, local(): lax.all_gather(own_query.reshape(batch_rows, heads_dev * HD), 'tp', axis=...  21 us
    dot_general x1, matrix products, local(): projected = jnp.dot(head_rows, w_out, preferred_element_type=jnp.float32)  8.86 us
    dot_general x1, matrix products, local(): query_wide = jnp.dot(normed_in, w_query, preferred_element_type=jnp.float32)  8.74 us
  transfers between devices with their start and end apart: 7, of which 5 were waited for; matrix products, arithmetic and copies ran while one was open for 4% of the time, Pallas kernels for 0%

profile of v1, /device:TPU:0, one launch (start us, length us, event | category | flops | bytes accessed | tf_op | source)
XLA Modules:
  0.0 425.5 jit_solution(3404575468552198465)
XLA Ops:
  8.0 0.8 convert_element_type.51
  9.4 0.7 broadcast_compare_fusion
  10.3 40.5 %all-gather.2.cloned.1.call-done = bf16[32,16384]{1,0:T(8,128)(2,1)} async-done(((bf16[32,1024]{1,0:T(8,128)(2,1)}), bf16[32,16384]{1,0:T(8,128)(2,1)}) %all-gather.2.cloned.1.call-update) | async-done | bytes 1048592 | tf_op jit(solution)/shard_map/all_gather | solution.py:43
  50.8 1.5 fusion
  52.3 1.5 fusion.2
  55.1 8.7 %fusion.31 = f32[32,512]{1,0:T(8,128)S(1)} fusion(bf16[32,16384]{1,0:T(8,128)(2,1)S(1)} %fusion.2, bf16[16384,512]{1,0:T(8,128)(2,1)} %param.12), kind=kOutput, calls=%fused_computation.59 | convolution fusion | flops 536870912 | bytes 17891328 | tf_op jit(solution)/shard_map/dot_general | solution.py:54
  64.1 21.0 %all_gather.7 = bf16[32,8192]{1,0:T(8,128)(2,1)S(1)} all-gather(bf16[32,512]{1,0:T(8,128)(2,1)S(1)} %bitcast.62), channel_id=1, replica_groups=mesh['replica'=2,'tp'=16] {'tp'}, dimensions={1}, use_global_device_ids=true | all-gather | bytes 557056 | tf_op jit(solution)/shard_map/all_gather | solution.py:56
  85.3 0.8 copy-done.3
  86.1 0.7 fusion.30
  86.8 58.8 %pmax.7 = f32[32,8,8]{2,1,0:T(8,128)S(1)} all-reduce(f32[32,8,8]{2,1,0:T(8,128)S(1)} %get-tuple-element.18), channel_id=1, replica_groups=mesh['replica'=2,'tp'=16] {'tp'}, use_global_device_ids=true, to_apply=%region_2.0 | all-reduce | flops 2048 | bytes 16384 | tf_op jit(solution)/shard_map/pmax | solution.py:76
  145.6 1.2 subtract_convert_fusion
  146.9 1.4 fusion.15
  149.5 1.6 copy.27
  152.5 2.1 fusion.17
  154.6 0.7 copy.29
  156.0 59.6 %all-reduce.6 = (f32[32,64]{0,1:T(8,128)S(1)}, bf16[32,1024]{1,0:T(8,128)(2,1)S(1)}) all-reduce(f32[32,64]{0,1:T(8,128)S(1)} %bitcast.60, f32[32,1024]{1,0:T(8,128)S(1)} %fusion.17), channel_id=3, replica_groups=mesh['replica'=2,'tp'=16] {'tp'}, use_global_device_ids=true, to_apply=%region_7.8.clone | all-reduce | flops 34816 | bytes 212992
  215.7 1.0 copy.28
  216.7 0.7 fusion.27
  217.4 8.9 %fusion.20 = f32[32,16384]{1,0:T(8,128)S(1)} fusion(bf16[512,16384]{1,0:T(8,128)(2,1)} %param.15, f32[32,4]{0,1:T(4,128)S(1)} %get-tuple-element.15, f32[32,4,128]{2,0,1:T(8,128)} %reduce-scatter.2.cloned.1.call-done, f32[32,128]{1,0:T(8,128)S(1)} %bitcast.59, f32[32,4]{0,1:T(4,128)S(1)} %convert_element_type.57), kind=kOutput, calls=%fused_computation.37 | convolution fusion | flops 536936448 | bytes 18957312 | tf_op jit(solution)/shard_map/dot_general | solution.py:109
  226.3 4.2 collective-permute-done
  230.7 47.7 %collective-permute-done.1 = f32[32,16384]{1,0:T(8,128)S(1)} collective-permute-done((f32[32,16384]{1,0:T(8,128)S(1)}, f32[32,16384]{1,0:T(8,128)S(1)}, u32[]{:S(2)}, u32[]{:S(2)}) %collective-permute-start.1) | collective-permute-done | bytes 2097184 | tf_op jit(solution)/shard_map/ppermute | solution.py:112
  278.7 46.8 %collective-permute-done.2 = f32[32,16384]{1,0:T(8,128)S(1)} collective-permute-done((f32[32,16384]{1,0:T(8,128)S(1)}, f32[32,16384]{1,0:T(8,128)S(1)}, u32[]{:S(2)}, u32[]{:S(2)}) %collective-permute-start.2) | collective-permute-done | bytes 2097184 | tf_op jit(solution)/shard_map/ppermute | solution.py:112
  326.0 91.8 %collective-permute-done.3 = f32[32,16384]{1,0:T(8,128)S(1)} collective-permute-done((f32[32,16384]{1,0:T(8,128)S(1)}, f32[32,16384]{1,0:T(8,128)S(1)}, u32[]{:S(2)}, u32[]{:S(2)}) %collective-permute-start.3) | collective-permute-done | bytes 2097184 | tf_op jit(solution)/shard_map/ppermute | solution.py:112
  418.2 0.7 multiply_convert_fusion
  (54 shorter events, 7.4 us)
Async XLA Ops:
  7.2 46.7 %copy-start = (bf16[1024,1024]{1,0:T(8,128)(2,1)S(1)}, bf16[1024,1024]{1,0:T(8,128)(2,1)}, u32[]{:S(2)}) copy-start(bf16[1024,1024]{1,0:T(8,128)(2,1)} %param.13) | copy-start | bytes 6291460
  7.2 43.6 %all-gather.2.cloned.1.call-start = ((), (), s32[]{:S(2)}) async-start(), calls=%async_computation.1 | async-start | bytes 1114112 | tf_op jit(solution)/shard_map/all_gather | solution.py:43
  7.9 137.7 %all-reduce.5.cloned.1.call-start = ((), (), s32[]{:S(2)}) async-start(), calls=%async_computation.2 | async-start | bytes 262144 | tf_op jit(solution)/shard_map/psum | solution.py:51
  53.9 10.0 %copy-start.2 = (bf16[32,16384]{1,0:T(8,128)(2,1)}, bf16[32,16384]{1,0:T(8,128)(2,1)S(1)}, u32[]{:S(2)}) copy-start(bf16[32,16384]{1,0:T(8,128)(2,1)S(1)} %fusion.2) | copy-start | bytes 3145732
  55.1 162.4 %reduce-scatter.2.cloned.1.call-start = ((), (), s32[]{:S(2)}) async-start(), calls=%async_computation.3 | async-start | bytes 1114112 | tf_op jit(solution)/shard_map/reduce_scatter | solution.py:86
  63.9 22.2 %copy-start.4 = (bf16[32,16,1024]{2,1,0:T(8,128)(2,1)S(1)}, bf16[32,16,1024]{2,1,0:T(8,128)(2,1)}, u32[]{:S(2)}) copy-start(bf16[32,16,1024]{2,1,0:T(8,128)(2,1)} %param.16) | copy-start | bytes 3145732
  85.2 0.8 copy-start.3
  145.6 3.4 copy-start.5
  149.5 1.7 copy-start.7
  226.3 4.2 collective-permute-start
  230.7 47.7 %collective-permute-start.1 = (f32[32,16384]{1,0:T(8,128)S(1)}, f32[32,16384]{1,0:T(8,128)S(1)}, u32[]{:S(2)}, u32[]{:S(2)}) collective-permute-start(f32[32,16384]{1,0:T(8,128)S(1)} %add.83), channel_id=1, source_target_pairs={{0,2},{1,3},{2,0},{3,1},{4,6},{5,7},{6,4},{7,5},{8,10},{9,11},{10,... | collective-permute-start | bytes 6291464 | tf_op jit(solution)/shard_map/ppermute | solution.py:112
  278.6 47.3 %copy-start.6 = (bf16[1024]{0:T(1024)(128)(2,1)S(1)}, bf16[1024]{0:T(1024)(128)(2,1)}, u32[]{:S(2)}) copy-start(bf16[1024]{0:T(1024)(128)(2,1)} %param.19) | copy-start | bytes 6148
  278.6 139.1 %copy-start.1 = (bf16[32,16384]{1,0:T(8,128)(2,1)S(1)}, bf16[32,16384]{1,0:T(8,128)(2,1)}, u32[]{:S(2)}) copy-start(bf16[32,16384]{1,0:T(8,128)(2,1)} %all-gather.2.cloned.1.call-done) | copy-start | bytes 3145732
  278.6 46.9 %collective-permute-start.2 = (f32[32,16384]{1,0:T(8,128)S(1)}, f32[32,16384]{1,0:T(8,128)S(1)}, u32[]{:S(2)}, u32[]{:S(2)}) collective-permute-start(f32[32,16384]{1,0:T(8,128)S(1)} %add.84), channel_id=1, source_target_pairs={{0,4},{1,5},{2,6},{3,7},{4,0},{5,1},{6,2},{7,3},{8,12},{9,13},{10,... | collective-permute-start | bytes 6291464 | tf_op jit(solution)/shard_map/ppermute | solution.py:112
  325.9 91.9 %collective-permute-start.3 = (f32[32,16384]{1,0:T(8,128)S(1)}, f32[32,16384]{1,0:T(8,128)S(1)}, u32[]{:S(2)}, u32[]{:S(2)}) collective-permute-start(f32[32,16384]{1,0:T(8,128)S(1)} %add.85), channel_id=1, source_target_pairs={{0,8},{1,9},{2,10},{3,11},{4,12},{5,13},{6,14},{7,15},{8,0},{9,1},... | collective-permute-start | bytes 6291464 | tf_op jit(solution)/shard_map/ppermute | solution.py:112
Sparse Core Ops, SparseCore 0:
  10.2 40.5 all-gather.1
  55.2 87.4 all-reduce.4
  151.3 56.6 reduce-scatter.1
